TPU v7x, 32 devices: a whole 2x2x4 slice. The times are simulated.
32 devices in a mesh: dp: 4 (over z), feat: 8 (over y, x, core).
Axes of the slice: x: 2, y: 2, z: 4, core: 2. Of those that a mesh axis runs over, the one named last changes fastest.
Arguments:
- features: float32 [4096, 8192], P('dp', 'feat'), may hold values from -0.0625 to 0.0625
- labels: int32 [4096], P('dp'), may hold values from -1 to 1, as said below
- weights: float32 [8192], P('feat'), may hold values from -6 to 6
Outputs:
- gradient: float32 [8192], P('feat')
- newton_step: float32 [8192], P('feat')
- residual: float32 [8192], P('feat')
Inputs may be any that keep to these rules, and one draw needn't show every extreme that they name: `labels`: every label is -1 or +1.
All inputs are finite; a program needn't handle non-finite values.
Results may differ from a plain program's by a relative error of at most 0.0003.
Values sent between devices are 32-bit elements; how exact they have to be, the bound alone decides.
A program may use at most 64 MiB of HBM per device.

v0:
```python
import jax
import jax.numpy as jnp
from jax import lax
from jax.sharding import PartitionSpec as P

CG_STEPS = 3


PENALTY = 4.0
HIGH = lax.Precision.HIGHEST


def squares(residual):
    return lax.psum(jnp.sum(residual * residual), "feat")


def local(features, labels, weights):
    y = labels.astype(jnp.float32)
    margin = y * lax.psum(jnp.dot(features, weights, precision=HIGH), "feat")
    sig = 1.0 / (1.0 + jnp.exp(-margin))
    local_grad = jnp.dot((sig - 1.0) * y, features, precision=HIGH)
    gradient = weights + PENALTY * lax.psum(local_grad, "dp")
    curv = PENALTY * sig * (1.0 - sig)
    newton_step = jnp.zeros_like(weights)
    residual = -gradient
    direction = residual
    rr = squares(residual)
    for step in range(CG_STEPS):
        image_rows, dir_sq = lax.psum(
            (jnp.dot(features, direction, precision=HIGH), jnp.sum(direction * direction)), "feat"
        )
        weighted = curv * image_rows
        back, quad = lax.psum(
            (jnp.dot(weighted, features, precision=HIGH), jnp.sum(weighted * image_rows)), "dp"
        )
        curvature = dir_sq + quad
        image = direction + back
        alpha = rr / curvature
        newton_step = newton_step + alpha * direction
        residual = residual - alpha * image
        fresh = squares(residual)
        direction = residual + fresh / rr * direction
        rr = fresh
    return (gradient, newton_step, residual)


def solution(mesh):
    placed = (P("dp", "feat"), P("dp"), P("feat"))
    return jax.shard_map(
        local,
        mesh=mesh,
        in_specs=placed,
        out_specs=(P("feat"), P("feat"), P("feat")),
        check_vma=False,
    )
```

profile of v0, /device:TPU:0, one launch (start us, length us, event | category | flops | bytes accessed | tf_op | source)
XLA Modules:
  0.0 174.1 jit_solution(13997829717275814949)
XLA Ops:
  0.7 5.8 %fusion.3 = f32[1,1024]{1,0:T(1,128)S(1)} fusion(f32[1024,1024]{1,0:T(8,128)} %param.3, f32[1024,1]{0,1:T(1,128)} %bitcast.34), kind=kOutput, calls=%fused_computation.21 | convolution fusion | flops 12582912 | bytes 4202496 | tf_op jit(solution)/shard_map/dot_general | solution.py:19
  6.4 15.2 %psum.115 = f32[1024]{0:T(1024)S(1)} all-reduce(f32[1024]{0:T(1024)S(1)} %bitcast.45), channel_id=1, replica_groups=mesh['dp'=4,'feat'=8] {'feat'}, use_global_device_ids=true, to_apply=%region_0.0 | all-reduce | flops 1024 | bytes 8192 | tf_op jit(solution)/shard_map/psum | solution.py:19
  21.6 4.3 %fusion.4 = f32[1,1024]{1,0:T(1,128)S(1)} fusion(f32[1024,1]{0,1:T(1,128)S(1)} %bitcast.47, f32[1024,1024]{1,0:T(8,128)} %param.3), kind=kOutput, calls=%fused_computation.22 | convolution fusion | flops 12582912 | bytes 4202496 | tf_op jit(solution)/shard_map/dot_general | solution.py:21
  25.9 11.9 %psum.116 = f32[1024]{0:T(1024)S(1)} all-reduce(f32[1024]{0:T(1024)S(1)} %bitcast.44), channel_id=1, replica_groups=mesh['dp'=4,'feat'=8] {'dp'}, use_global_device_ids=true, to_apply=%region_1.0 | all-reduce | flops 1024 | bytes 8192 | tf_op jit(solution)/shard_map/psum | solution.py:22
  38.4 5.6 %fusion.5 = f32[1,1024]{1,0:T(1,128)S(1)} fusion(f32[1024,1]{0,1:T(1,128)S(1)} %bitcast.46, f32[1024,1024]{1,0:T(8,128)} %param.3), kind=kOutput, calls=%fused_computation.23 | convolution fusion | flops 12582912 | bytes 4202496 | tf_op jit(solution)/shard_map/dot_general | solution.py:30
  44.1 12.8 %all-reduce.2 = (f32[1024]{0:T(1024)S(1)}, f32[]{:T(128)}) all-reduce(f32[1024]{0:T(1024)S(1)} %bitcast.38, f32[]{:T(128)} %get-tuple-element.21), channel_id=1, replica_groups=mesh['dp'=4,'feat'=8] {'feat'}, use_global_device_ids=true, to_apply=%region_4.0 | all-reduce | flops 1025 | bytes 8200 | tf_op jit(solution)/shard_map/psum | solution.py:29
  57.4 4.3 %fusion.6 = f32[1,1024]{1,0:T(1,128)S(1)} fusion(f32[1024,1]{0,1:T(1,128)S(1)} %bitcast.36, f32[1024,1024]{1,0:T(8,128)} %param.3), kind=kOutput, calls=%fused_computation.24 | convolution fusion | flops 12582912 | bytes 4202496 | tf_op jit(solution)/shard_map/dot_general | solution.py:34
  61.7 9.1 %all-reduce.5 = (f32[1024]{0:T(1024)S(1)}, f32[]{:T(128)}) all-reduce(f32[1024]{0:T(1024)S(1)} %bitcast.39, f32[]{:T(128)} %get-tuple-element.29), channel_id=1, replica_groups=mesh['dp'=4,'feat'=8] {'dp'}, use_global_device_ids=true, to_apply=%region_7.0 | all-reduce | flops 1025 | bytes 8200 | tf_op jit(solution)/shard_map/psum | solution.py:33
  72.7 0.6 multiply_reduce_fusion.5
  73.3 12.6 %psum.121 = f32[]{:T(128)} all-reduce(f32[]{:T(128)} %multiply_reduce_fusion.5), channel_id=1, replica_groups=mesh['dp'=4,'feat'=8] {'feat'}, use_global_device_ids=true, to_apply=%region_9.0 | all-reduce | flops 1 | bytes 8 | tf_op jit(solution)/shard_map/psum | solution.py:14
  87.3 0.6 multiply_reduce_fusion.4
  87.9 5.6 %fusion.7 = f32[1,1024]{1,0:T(1,128)S(1)} fusion(f32[1024,1]{0,1:T(1,128)S(1)} %bitcast.32, f32[1024,1024]{1,0:T(8,128)} %param.3), kind=kOutput, calls=%fused_computation.25 | convolution fusion | flops 12582912 | bytes 4202496 | tf_op jit(solution)/shard_map/dot_general | solution.py:30
  93.5 12.8 %all-reduce.1 = (f32[1024]{0:T(1024)S(1)}, f32[]{:T(128)}) all-reduce(f32[1024]{0:T(1024)S(1)} %bitcast.42, f32[]{:T(128)} %get-tuple-element.19), channel_id=1, replica_groups=mesh['dp'=4,'feat'=8] {'feat'}, use_global_device_ids=true, to_apply=%region_12.0 | all-reduce | flops 1025 | bytes 8200 | tf_op jit(solution)/shard_map/psum | solution.py:29
  106.3 0.7 multiply_reduce_fusion.3
  107.0 4.3 %fusion.8 = f32[1,1024]{1,0:T(1,128)S(1)} fusion(f32[1024,1]{0,1:T(1,128)S(1)} %bitcast.37, f32[1024,1024]{1,0:T(8,128)} %param.3), kind=kOutput, calls=%fused_computation.26 | convolution fusion | flops 12582912 | bytes 4202496 | tf_op jit(solution)/shard_map/dot_general | solution.py:34
  111.2 11.1 %all-reduce.4 = (f32[1024]{0:T(1024)S(1)}, f32[]{:T(128)}) all-reduce(f32[1024]{0:T(1024)S(1)} %bitcast.40, f32[]{:T(128)} %get-tuple-element.27), channel_id=1, replica_groups=mesh['dp'=4,'feat'=8] {'dp'}, use_global_device_ids=true, to_apply=%region_15.0 | all-reduce | flops 1025 | bytes 8200 | tf_op jit(solution)/shard_map/psum | solution.py:33
  124.2 0.6 multiply_reduce_fusion.2
  124.8 12.4 %psum.126 = f32[]{:T(128)} all-reduce(f32[]{:T(128)} %get-tuple-element.17), channel_id=1, replica_groups=mesh['dp'=4,'feat'=8] {'feat'}, use_global_device_ids=true, to_apply=%region_17.0 | all-reduce | flops 1 | bytes 8 | tf_op jit(solution)/shard_map/psum | solution.py:14
  139.2 5.6 %fusion.9 = f32[1,1024]{1,0:T(1,128)S(1)} fusion(f32[1024,1]{0,1:T(1,128)S(1)} %bitcast.33, f32[1024,1024]{1,0:T(8,128)} %param.3), kind=kOutput, calls=%fused_computation.27 | convolution fusion | flops 12582912 | bytes 4202496 | tf_op jit(solution)/shard_map/dot_general | solution.py:30
  144.8 12.7 %all-reduce = (f32[]{:T(128)}, f32[1024]{0:T(1024)S(1)}) all-reduce(f32[]{:T(128)} %get-tuple-element.15, f32[1024]{0:T(1024)S(1)} %bitcast.43), channel_id=1, replica_groups=mesh['dp'=4,'feat'=8] {'feat'}, use_global_device_ids=true, to_apply=%region_19.0 | all-reduce | flops 1025 | bytes 8200 | tf_op jit(solution)/shard_map/psum | solution.py:29
  157.6 0.7 fusion
  158.3 4.3 %fusion.10 = f32[1,1024]{1,0:T(1,128)S(1)} fusion(f32[1024,1]{0,1:T(1,128)S(1)} %bitcast.35, f32[1024,1024]{1,0:T(8,128)} %param.3), kind=kOutput, calls=%fused_computation.28 | convolution fusion | flops 12582912 | bytes 4202496 | tf_op jit(solution)/shard_map/dot_general | solution.py:34
  162.5 9.1 %all-reduce.3 = (f32[]{:T(128)}, f32[1024]{0:T(1024)S(1)}) all-reduce(f32[]{:T(128)} %get-tuple-element.26, f32[1024]{0:T(1024)S(1)} %bitcast.41), channel_id=1, replica_groups=mesh['dp'=4,'feat'=8] {'dp'}, use_global_device_ids=true, to_apply=%region_22.0 | all-reduce | flops 1025 | bytes 8200 | tf_op jit(solution)/shard_map/psum | solution.py:33
  173.5 0.6 multiply_subtract_fusion
  (11 shorter events, 1.8 us)
Async XLA Ops:
  0.6 20.9 %copy-start.2 = (s32[1024]{0:T(1024)S(1)}, s32[1024]{0:T(1024)}, u32[]{:S(2)}) copy-start(s32[1024]{0:T(1024)} %param.4) | copy-start | bytes 12292
  0.6 37.2 %copy-start.1 = (f32[1024]{0:T(1024)S(1)}, f32[1024]{0:T(1024)}, u32[]{:S(2)}) copy-start(f32[1024]{0:T(1024)} %param.5) | copy-start | bytes 12292
  38.4 135.1 %copy-start = (f32[1024]{0:T(1024)}, f32[1024]{0:T(1024)S(1)}, u32[]{:S(2)}) copy-start(f32[1024]{0:T(1024)S(1)} %get-tuple-element.22) | copy-start | bytes 12292
where the time goes:
time: 175 us; the launch traced here: 174 us
  blocking collectives  120 us (69%)
  matrix products  39.8 us (23%)
  between operations  9.03 us (5%)
  other arithmetic  5.6 us (3%)
    psum x3, blocking collectives, local(): lax.psum((jnp.dot(features, direction, precision=HIGH), jnp.sum(direction...  38.2 us
    psum x3, blocking collectives, local(): lax.psum((jnp.dot(weighted, features, precision=HIGH), jnp.sum(weighted *...  29.4 us
    psum x2, blocking collectives, squares(): return lax.psum(jnp.sum(residual * residual), 'feat')  25 us
    dot_general x3, matrix products, local(): jnp.dot(features, direction, precision=HIGH)  16.9 us
    psum x1, blocking collectives, local(): margin = y * lax.psum(jnp.dot(features, weights, precision=HIGH), 'feat')  15.2 us
    dot_general x3, matrix products, local(): jnp.dot(weighted, features, precision=HIGH)  12.8 us
    psum x1, blocking collectives, local(): gradient = weights + PENALTY * lax.psum(local_grad, 'dp')  11.9 us
    dot_general x1, matrix products, local(): margin = y * lax.psum(jnp.dot(features, weights, precision=HIGH), 'feat')  5.76 us

commit v1 on v0

v1 whole, which is shorter than its diff:
```python
import functools

import jax
import jax.numpy as jnp
from jax import lax
from jax.experimental import pallas as pl
from jax.experimental.pallas import tpu as pltpu
from jax.sharding import PartitionSpec as P

CG_STEPS = 3
ROUNDS = CG_STEPS + 1
PENALTY = 4.0
MESH = pl.DeviceIdType.MESH
LANES = 128
SUBLANES = 8
CHUNK = 128


def class_order(labels):
    rows = labels.shape[0]
    wide = rows * LANES // SUBLANES
    per = LANES // SUBLANES
    source = labels.astype(jnp.bfloat16)
    lane = lax.broadcasted_iota(jnp.int32, (LANES, wide), 0)
    column = lax.broadcasted_iota(jnp.int32, (LANES, wide), 1)
    row = lax.broadcasted_iota(jnp.int32, (rows, wide), 0)
    keep = row == lax.broadcasted_iota(jnp.int32, (rows, wide), 1) // per
    out = []
    for s in range(SUBLANES):
        pick = (lane == SUBLANES * (column % per) + s).astype(jnp.float32).astype(jnp.bfloat16)
        moved = jnp.dot(source, pick, preferred_element_type=jnp.float32)
        out.append(jnp.sum(jnp.where(keep, moved, 0.0), axis=0, keepdims=True))
    return jnp.concatenate(out, axis=0)


def kernel(nd, nf, x_hbm, labels_ref, weights_ref, grad_ref, newton_ref, resid_ref,
           x, vec, f_out, f_in, fx_out, fx_in, d_out, d_in, dx_out, dx_in,
           load_sem, fs, fr, fxs, fxr, ds, dr, dxs, dxr):
    samples, width = x.shape
    blocks = width // LANES
    chunks = samples // CHUNK
    per = CHUNK // SUBLANES
    my_f, my_d = lax.axis_index("feat"), lax.axis_index("dp")

    loads = []
    for c in range(chunks):
        rows = pl.ds(c * CHUNK, CHUNK)
        load = pltpu.make_async_copy(x_hbm.at[rows], x.at[rows], load_sem.at[c])
        load.start()
        loads.append(load)

    barrier = pltpu.get_barrier_semaphore()
    for k in range(1, nf):
        pl.semaphore_signal(barrier, inc=1, device_id={"feat": lax.rem(my_f + k, nf)}, device_id_type=MESH)
    for k in range(1, nd):
        pl.semaphore_signal(barrier, inc=1, device_id={"dp": lax.rem(my_d + k, nd)}, device_id_type=MESH)

    pending = []

    def publish(axis, me, n, out, inbox, send, recv, value, step):
        out[step] = value
        inbox[step, me] = value
        for k in range(n - 1, 0, -1):
            copy = pltpu.make_async_remote_copy(
                src_ref=out.at[step],
                dst_ref=inbox.at[step, me],
                send_sem=send.at[step, k],
                recv_sem=recv.at[step, me],
                device_id={axis: lax.rem(me + k, n)},
                device_id_type=MESH,
            )
            copy.start()
            pending.append(copy)

    def collect(axis, me, n, out, inbox, send, recv, step):
        for k in range(1, n):
            peer = lax.rem(me + k, n)
            pltpu.make_async_remote_copy(
                src_ref=out.at[step],
                dst_ref=inbox.at[step, peer],
                send_sem=send.at[step, k],
                recv_sem=recv.at[step, peer],
                device_id={axis: peer},
                device_id_type=MESH,
            ).wait_recv()
        parts = [inbox[step, i] for i in range(n)]
        while len(parts) > 1:
            parts = [sum(parts[i + 1 : i + 2], parts[i]) for i in range(0, len(parts), 2)]
        return parts[0]

    feat = ("feat", my_f, nf, f_out, f_in, fs, fr)
    feat_x = ("feat", my_f, nf, fx_out, fx_in, fxs, fxr)
    dp = ("dp", my_d, nd, d_out, d_in, ds, dr)
    dp_x = ("dp", my_d, nd, dx_out, dx_in, dxs, dxr)

    lane = lax.broadcasted_iota(jnp.int32, (SUBLANES, samples // SUBLANES), 1)

    def forward(v, first=False):
        total = jnp.zeros((SUBLANES, samples // SUBLANES), jnp.float32)
        rows_of = [jnp.broadcast_to(v[k : k + 1, :], (CHUNK, LANES)) for k in range(blocks)]
        for c in range(chunks):
            if first:
                loads[c].wait()
            part = None
            for k in range(blocks):
                term = x[c * CHUNK : (c + 1) * CHUNK, k * LANES : (k + 1) * LANES] * rows_of[k]
                part = term if part is None else part + term
            sums = jnp.sum(part, axis=1, keepdims=True)
            for j in range(per):
                piece = jnp.broadcast_to(sums[j * SUBLANES : (j + 1) * SUBLANES], total.shape)
                total = jnp.where(lane == c * per + j, piece, total)
        return total

    def backward(u):
        acc = [jnp.zeros((SUBLANES, LANES), jnp.float32)] * blocks
        for c in range(chunks):
            wide = [
                jnp.broadcast_to(u[:, c * per + j : c * per + j + 1], (SUBLANES, LANES)) for j in range(per)
            ]
            for k in range(blocks):
                for j in range(per):
                    top = c * CHUNK + j * SUBLANES
                    acc[k] = acc[k] + x[top : top + SUBLANES, k * LANES : (k + 1) * LANES] * wide[j]
        return jnp.concatenate([jnp.sum(a, axis=0, keepdims=True) for a in acc], axis=0)

    def whole(row):
        return jnp.sum(row, axis=1, keepdims=True)

    def fold(a):
        return jnp.sum(a, axis=0, keepdims=True)

    weights = weights_ref[...]
    margin_part = forward(weights, first=True)
    pl.semaphore_wait(barrier, nf - 1 + nd - 1)
    publish(*feat, margin_part, 0)
    y = class_order(labels_ref[...])
    margin = y * collect(*feat, 0)
    sig = 1.0 / (1.0 + jnp.exp(-margin))
    publish(*dp, backward((sig - 1.0) * y), 0)
    curv = PENALTY * sig * (1.0 - sig)
    gradient = weights + PENALTY * collect(*dp, 0)
    grad_ref[...] = gradient

    residual = -gradient
    direction = residual
    newton = jnp.zeros_like(gradient)
    rr = dir_sq = image_rows = None
    for step in range(1, ROUNDS):
        squares = fold(residual * residual)
        cross = fold(residual * direction)
        publish(*feat_x, jnp.concatenate([squares, cross], axis=0), step - 1)
        publish(*feat, forward(residual), step)
        sums = collect(*feat_x, step - 1)
        fresh = whole(sums[0:1])
        mixed = whole(sums[1:2])
        res_rows = collect(*feat, step)
        if step == 1:
            dir_sq, image_rows = fresh, res_rows
        else:
            beta = fresh / rr
            direction = residual + beta * direction
            image_rows = res_rows + beta * image_rows
            dir_sq = fresh + beta * (2.0 * mixed + beta * dir_sq)
        rr = fresh
        weighted = curv * image_rows
        publish(*dp_x, fold(weighted * image_rows), step - 1)
        publish(*dp, backward(weighted), step)
        quad = whole(collect(*dp_x, step - 1))
        alpha = rr / (dir_sq + quad)
        back = collect(*dp, step)
        newton = newton + alpha * direction
        residual = residual - alpha * (direction + back)
    newton_ref[...] = newton
    resid_ref[...] = residual
    for copy in pending:
        copy.wait_send()


def solution(mesh):
    nd, nf = mesh.shape["dp"], mesh.shape["feat"]
    placed = (P("dp", "feat"), P("dp"), P("feat"))

    def local(features, labels, weights):
        samples, width = features.shape
        blocks = width // LANES
        compact = (SUBLANES, samples // SUBLANES)
        rows = (blocks, LANES)
        f32 = jnp.float32
        dma = pltpu.SemaphoreType.DMA
        vmem = pl.BlockSpec(memory_space=pltpu.VMEM)
        outs = pl.pallas_call(
            functools.partial(kernel, nd, nf),
            out_shape=[jax.ShapeDtypeStruct(rows, f32)] * 3,
            in_specs=[pl.BlockSpec(memory_space=pl.ANY), vmem, vmem],
            out_specs=[vmem] * 3,
            scratch_shapes=[
                pltpu.VMEM((samples, width), f32),
                pltpu.VMEM(rows, f32),
                pltpu.VMEM((ROUNDS,) + compact, f32),
                pltpu.VMEM((ROUNDS, nf) + compact, f32),
                pltpu.VMEM((CG_STEPS, 2, LANES), f32),
                pltpu.VMEM((CG_STEPS, nf, 2, LANES), f32),
                pltpu.VMEM((ROUNDS,) + rows, f32),
                pltpu.VMEM((ROUNDS, nd) + rows, f32),
                pltpu.VMEM((CG_STEPS, 1, samples // SUBLANES), f32),
                pltpu.VMEM((CG_STEPS, nd, 1, samples // SUBLANES), f32),
                dma((samples // CHUNK,)),
                dma((ROUNDS, nf)),
                dma((ROUNDS, nf)),
                dma((CG_STEPS, nf)),
                dma((CG_STEPS, nf)),
                dma((ROUNDS, nd)),
                dma((ROUNDS, nd)),
                dma((CG_STEPS, nd)),
                dma((CG_STEPS, nd)),
            ],
            compiler_params=pltpu.CompilerParams(
                collective_id=0, has_side_effects=True, vmem_limit_bytes=60 * 1024 * 1024
            ),
        )(features, labels.reshape(samples // LANES, LANES), weights.reshape(rows))
        return tuple(out.reshape(width) for out in outs)

    return jax.shard_map(
        local,
        mesh=mesh,
        in_specs=placed,
        out_specs=(P("feat"), P("feat"), P("feat")),
        check_vma=False,
    )
```

time: 175 us -> 42.4 us (0.24)
  blocking collectives: 120 us -> 0 us
  matrix products: 39.8 us -> 0 us
  Pallas kernels: 0 us -> 37.6 us
  between operations: 9.03 us -> 0.64 us
  other arithmetic: 5.6 us -> 0 us
  local copies, waits for them, and re-layouts: 0.01 us -> 3.8 us
    psum x10 -> x0, blocking collectives: 120 us -> none  [the longest x3 38.2 us: local(): lax.psum((jnp.dot(features, direction, precision=HIGH), jnp.sum(direction...]
    dot_general x8 -> x0, matrix products: 39.8 us -> none  [the longest x3 16.9 us: local(): jnp.dot(features, direction, precision=HIGH)]
    pallas_call x0 -> x1, Pallas kernels: none -> 37.6 us  [local(): pl.pallas_call(functools.partial(kernel, nd, nf), out_shape=[jax.ShapeDty...]
    reduce_sum x7 -> x0, other arithmetic: 4.3 us -> none  [the longest x3 1.81 us: squares(): return lax.psum(jnp.sum(residual * residual), 'feat')]
    unnamed x6 -> x3, local copies, waits for them, and re-layouts: 0.01 us -> 3.8 us
where the time goes in v1:
time: 42.4 us; the launch traced here: 42.1 us
  Pallas kernels  37.6 us (89%)
  local copies, waits for them, and re-layouts  3.8 us (9%)
  between operations  0.64 us (2%)
    pallas_call x1, Pallas kernels, local(): pl.pallas_call(functools.partial(kernel, nd, nf), out_shape=[jax.ShapeDty...  37.6 us
    unnamed x3, local copies, waits for them, and re-layouts  3.8 us

profile of v1, /device:TPU:0, one launch (start us, length us, event | category | flops | bytes accessed | tf_op | source)
XLA Modules:
  0.0 42.1 jit_solution(10729559754305602987)
XLA Ops:
  0.6 37.6 %shard_map.58 = (f32[8,128]{1,0:T(8,128)}, f32[8,128]{1,0:T(8,128)}, f32[8,128]{1,0:T(8,128)}) custom-call(f32[1024,1024]{1,0:T(8,128)} %x_hbm.1, s32[8,128]{1,0:T(8,128)} %bitcast.8, f32[8,128]{1,0:T(8,128)} %bitcast.9), custom_call_target="tpu_custom_call" | custom-call | tf_op jit(solution)/shard_map/pallas_call | solution.py:191
  38.3 1.3 %copy.9 = f32[1024]{0:T(1024)} copy(f32[1024]{0:T(1024)} %bitcast.7) | data formatting | bytes 8192
  39.5 1.3 %copy.10 = f32[1024]{0:T(1024)} copy(f32[1024]{0:T(1024)} %bitcast.6) | data formatting | bytes 8192
  40.8 1.3 %copy.11 = f32[1024]{0:T(1024)} copy(f32[1024]{0:T(1024)} %bitcast.5) | data formatting | bytes 8192

commit v2 on v1

--- a/solution.py
+++ b/solution.py
@@ -33,7 +33,7 @@
     return jnp.concatenate(out, axis=0)
 
 
-def kernel(nd, nf, x_hbm, labels_ref, weights_ref, grad_ref, newton_ref, resid_ref,
+def kernel(nd, nf, x_hbm, labels_ref, weights_ref, out_ref,
            x, vec, f_out, f_in, fx_out, fx_in, d_out, d_in, dx_out, dx_in,
            load_sem, fs, fr, fxs, fxr, ds, dr, dxs, dxr):
     samples, width = x.shape
@@ -139,7 +139,7 @@
     publish(*dp, backward((sig - 1.0) * y), 0)
     curv = PENALTY * sig * (1.0 - sig)
     gradient = weights + PENALTY * collect(*dp, 0)
-    grad_ref[...] = gradient
+    out_ref[0] = gradient
 
     residual = -gradient
     direction = residual
@@ -170,8 +170,8 @@
         back = collect(*dp, step)
         newton = newton + alpha * direction
         residual = residual - alpha * (direction + back)
-    newton_ref[...] = newton
-    resid_ref[...] = residual
+    out_ref[1] = newton
+    out_ref[2] = residual
     for copy in pending:
         copy.wait_send()
 
@@ -190,9 +190,9 @@
         vmem = pl.BlockSpec(memory_space=pltpu.VMEM)
         outs = pl.pallas_call(
             functools.partial(kernel, nd, nf),
-            out_shape=[jax.ShapeDtypeStruct(rows, f32)] * 3,
+            out_shape=jax.ShapeDtypeStruct((3,)+rows, f32),
             in_specs=[pl.BlockSpec(memory_space=pl.ANY), vmem, vmem],
-            out_specs=[vmem] * 3,
+            out_specs=vmem,
             scratch_shapes=[
                 pltpu.VMEM((samples, width), f32),
                 pltpu.VMEM(rows, f32),
@@ -218,7 +218,7 @@
                 collective_id=0, has_side_effects=True, vmem_limit_bytes=60 * 1024 * 1024
             ),
         )(features, labels.reshape(samples // LANES, LANES), weights.reshape(rows))
-        return tuple(out.reshape(width) for out in outs)
+        return tuple(outs[i].reshape(width) for i in range(3))
 
     return jax.shard_map(
         local,

time: 42.4 us -> 39.8 us (0.939)
  local copies, waits for them, and re-layouts: 3.8 us -> 1.29 us
    unnamed x3 -> x0, local copies, waits for them, and re-layouts: 3.8 us -> none
    another operation x0 -> x1, local copies, waits for them, and re-layouts: none -> 1.29 us  [local(): return tuple((outs[i].reshape(width) for i in range(3)))]
where the time goes in v2:
time: 39.8 us; the launch traced here: 39.6 us
  Pallas kernels  37.6 us (94%)
  local copies, waits for them, and re-layouts  1.29 us (3%)
  between operations  0.64 us (2%)
    pallas_call x1, Pallas kernels, local(): pl.pallas_call(functools.partial(kernel, nd, nf), out_shape=jax.ShapeDtyp...  37.6 us
    another operation x1, local copies, waits for them, and re-layouts, local(): return tuple((outs[i].reshape(width) for i in range(3)))  1.29 us

profile of v2, /device:TPU:0, one launch (start us, length us, event | category | flops | bytes accessed | tf_op | source)
XLA Modules:
  0.0 39.6 jit_solution(10527041342879070678)
XLA Ops:
  0.6 37.6 %shard_map.58 = f32[3,8,128]{2,1,0:T(8,128)} custom-call(f32[1024,1024]{1,0:T(8,128)} %x_hbm.1, s32[8,128]{1,0:T(8,128)} %bitcast.8, f32[8,128]{1,0:T(8,128)} %bitcast.9), custom_call_target="tpu_custom_call" | custom-call | tf_op jit(solution)/shard_map/pallas_call | solution.py:191
  38.3 1.3 %slice_bitcast_fusion = (f32[1024]{0:T(1024)}, f32[1024]{0:T(1024)}, f32[1024]{0:T(1024)}) fusion(f32[3,8,128]{2,1,0:T(8,128)} %shard_map.58), kind=kLoop, calls=%fused_computation | loop fusion | bytes 24576 | tf_op jit(solution)/shard_map/reshape;squeeze | solution.py:221
